TPU v7x, 32 devices: a whole 2x2x4 slice. The times are simulated.
32 devices in a mesh: groups: 2 (over x), blk: 8 (over z, y), rep: 2 (over core).
Axes of the slice: x: 2, y: 2, z: 4, core: 2. Of those that a mesh axis runs over, the one named last changes fastest.
Arguments:
- tokens: bfloat16 [2048, 7168], P(('groups', 'blk', 'rep')), parts along dimension 0, may hold values from -6 to 6
- router_scores: float32 [2048, 8], P(('groups', 'blk', 'rep')), parts along dimension 0, may hold values from -6 to 6
- expert_ids: int32 [2048, 8], P(('groups', 'blk', 'rep')), parts along dimension 0, may hold values from 0 to 255, as said below
- gate_weight: bfloat16 [7168, 4096], P(None, ('blk', 'rep')), may hold values from -0.0625 to 0.0625
- up_weight: bfloat16 [7168, 4096], P(None, ('blk', 'rep')), may hold values from -0.0625 to 0.0625
- down_weight: bfloat16 [4096, 7168], P(('blk', 'rep')), may hold values from -0.125 to 0.125
Outputs:
- moe_out: bfloat16 [2048, 7168], P(('groups', 'blk', 'rep')), parts along dimension 0
There are 2 independent parts, one for each index of `groups`. A program takes and returns all parts, laid end to end along the dimension named above; an argument that names none is the same for every part. Nothing has to cross between parts.
Inputs may be any that keep to these rules, and one draw needn't show every extreme that they name: `expert_ids`: each row names 8 different experts. In the rows of one device (aligned blocks of 64 rows) each expert below 2 is named by at most 2 rows, and in every draw one such expert is named by exactly 2 rows in every block.
All inputs are finite; a program needn't handle non-finite values.
Results may differ from a plain program's by a relative error of at most 0.0068.
Values may be sent and summed in bfloat16 or wider, within the bound.
A program may use at most 128 MiB of HBM per device.

v0:
```python
import functools

import jax
import jax.numpy as jnp
from jax import lax
from jax.experimental import pallas as pl
from jax.experimental.pallas import tpu as pltpu
from jax.sharding import PartitionSpec as P

FF = 2048
CAP = 2
MESH = pl.DeviceIdType.MESH

route_scale = 2.5


def kernel(
    blks, reps, experts, kchunks, nchunks,
    scores_hbm, ids_hbm, tok_hbm, gate_hbm, up_hbm, down_hbm, out_ref,
    scores_ref, ids_ref, tok, wg, wu, wd, packed, rows, keep, give, got, back, returned, weight_buf,
    route_sem, tok_sem, w_sem, d_sem, dsend, recv, fsend, ysend, xsend, xrecv, bsend, brecv,
):
    b = lax.axis_index("blk")
    r = lax.axis_index("rep")
    sib = 1 - r
    group = blks // experts
    half = group // 2
    width = tok.shape[1]
    slots = experts * CAP
    kc = width // kchunks
    nc = width // nchunks
    parity = lax.rem(b, 2)
    own_q = lax.div(b, 2)
    own_expert = lax.div(b, group)
    quads = blks // 2

    barrier = pltpu.get_barrier_semaphore()
    other = b + 1 - 2 * parity

    def greet(bb, rr):
        pl.semaphore_signal(
            barrier, inc=1, device_id={"blk": bb, "rep": rr}, device_id_type=MESH
        )

    @pl.loop(1, quads)
    def _(i):
        greet(2 * lax.rem(own_q + i, quads) + parity, r)

    greet(other, r)
    greet(b, sib)

    route_copies = (
        pltpu.make_async_copy(scores_hbm, scores_ref, route_sem.at[0]),
        pltpu.make_async_copy(ids_hbm, ids_ref, route_sem.at[1]),
    )
    for copy in route_copies:
        copy.start()
    tok_copy = pltpu.make_async_copy(tok_hbm, tok, tok_sem)
    tok_copy.start()

    def k_copies(k):
        at = pl.ds(k * kc, kc)
        return (
            pltpu.make_async_copy(gate_hbm.at[at, :], wg.at[at, :], w_sem.at[0, k]),
            pltpu.make_async_copy(up_hbm.at[at, :], wu.at[at, :], w_sem.at[1, k]),
        )

    def d_copy(n):
        at = pl.ds(n * nc, nc)
        return pltpu.make_async_copy(down_hbm.at[:, at], wd.at[:, at], d_sem.at[n])

    for k in range(kchunks):
        for copy in k_copies(k):
            copy.start()
    for n in range(nchunks):
        d_copy(n).start()

    for copy in route_copies:
        copy.wait()
    sig = jax.nn.sigmoid(scores_ref[...])
    gates = route_scale * sig / jnp.sum(sig, axis=0, keepdims=True)
    ids = ids_ref[...]
    t_count = ids.shape[1]
    slot = lax.broadcasted_iota(jnp.int32, (slots, t_count), 0)
    slot_expert = lax.div(slot, CAP)
    slot_rank = (slot - slot_expert * CAP).astype(jnp.float32)
    hit = jnp.zeros((slots, t_count), jnp.float32)
    weight = jnp.zeros((slots, t_count), jnp.float32)
    for j in range(ids.shape[0]):
        same = ids[j : j + 1, :] == slot_expert
        hit = hit + jnp.where(same, 1.0, 0.0)
        weight = weight + jnp.where(same, gates[j : j + 1, :], 0.0)
    row_i = lax.broadcasted_iota(jnp.int32, (t_count, t_count), 0)
    col_i = lax.broadcasted_iota(jnp.int32, (t_count, t_count), 1)
    upto = jnp.where(row_i <= col_i, 1.0, 0.0).astype(jnp.bfloat16)
    rank = jnp.dot(hit.astype(jnp.bfloat16), upto, preferred_element_type=jnp.float32) - 1.0
    placed = jnp.where(rank == slot_rank, hit, 0.0)
    tok_copy.wait()
    picked = jnp.dot(
        placed.astype(jnp.bfloat16), tok[...], preferred_element_type=jnp.float32
    ).astype(jnp.bfloat16)
    for e in range(experts):
        packed[e] = picked[e * CAP : (e + 1) * CAP, :]

    pl.semaphore_wait(barrier, quads + 1)

    def first(e, h):
        dst = e * group + 2 * h + parity
        copy = pltpu.make_async_remote_copy(
            src_ref=packed.at[e], dst_ref=rows.at[r, b],
            send_sem=dsend.at[e * half + h], recv_sem=recv.at[r, b],
            device_id={"blk": dst, "rep": r}, device_id_type=MESH,
        )
        return dst, copy

    own_copy = pltpu.make_async_copy(packed.at[own_expert], rows.at[r, b], recv.at[r, b])
    own_copy.start()

    @pl.loop(0, experts)
    def _(e):
        @pl.loop(0, half)
        def _(h):
            dst, copy = first(e, h)

            @pl.when(dst != b)
            def _():
                copy.start()

    slot_weight = placed * weight
    for j in range(slots):
        spread = jnp.where(row_i == col_i, slot_weight[j : j + 1, :], 0.0)
        weight_buf[:, j : j + 1] = jnp.sum(spread, axis=1, keepdims=True)

    def landed(rr, bb):
        return pltpu.make_async_copy(rows.at[rr, bb], rows.at[rr, bb], recv.at[rr, bb])

    def forward(bb, sems, dst_b, dst_r):
        return pltpu.make_async_remote_copy(
            src_ref=rows.at[r, bb], dst_ref=rows.at[r, bb],
            send_sem=sems.at[bb], recv_sem=recv.at[r, bb],
            device_id={"blk": dst_b, "rep": dst_r}, device_id_type=MESH,
        )

    @pl.loop(0, quads)
    def _(i):
        bb = 2 * lax.rem(own_q + i, quads) + parity
        landed(r, bb).wait()
        forward(bb, ysend, other, r).start()
        forward(bb, fsend, b, sib).start()

    @pl.loop(0, quads)
    def _(i):
        bb = 2 * lax.rem(own_q + i, quads) + 1 - parity
        landed(r, bb).wait()
        forward(bb, fsend, b, sib).start()

    @pl.loop(0, blks)
    def _(bb):
        landed(sib, bb).wait()

    m = reps * blks * CAP
    gate_acc = jnp.zeros((m, wg.shape[1]), jnp.float32)
    up_acc = jnp.zeros((m, wg.shape[1]), jnp.float32)
    for k in range(kchunks):
        for copy in k_copies(k):
            copy.wait()
        at = slice(k * kc, (k + 1) * kc)
        x = rows[:, :, :, at].reshape(m, kc)
        gate_acc = gate_acc + jnp.dot(x, wg[at, :], preferred_element_type=jnp.float32)
        up_acc = up_acc + jnp.dot(x, wu[at, :], preferred_element_type=jnp.float32)
    hidden = (gate_acc / (1.0 + jnp.exp(-gate_acc)) * up_acc).astype(jnp.bfloat16)

    mh = m // reps

    def swap(n):
        at = pl.ds(n * nc, nc)
        return pltpu.make_async_remote_copy(
            src_ref=give.at[:, at], dst_ref=got.at[:, at],
            send_sem=xsend.at[n], recv_sem=xrecv.at[n],
            device_id={"blk": b, "rep": sib}, device_id_type=MESH,
        )

    def send_back(n, bb):
        at = pl.ds(n * nc, nc)
        return pltpu.make_async_remote_copy(
            src_ref=back.at[bb, :, at], dst_ref=returned.at[b, :, at],
            send_sem=bsend.at[n, bb], recv_sem=brecv.at[n, b],
            device_id={"blk": bb, "rep": r}, device_id_type=MESH,
        )

    def keep_back(n):
        at = pl.ds(n * nc, nc)
        return pltpu.make_async_copy(
            back.at[b, :, at], returned.at[b, :, at], brecv.at[n, b]
        )

    for n in range(nchunks):
        d_copy(n).wait()
        at = slice(n * nc, (n + 1) * nc)
        part = jnp.dot(hidden, wd[:, at], preferred_element_type=jnp.float32)
        low, high = part[:mh], part[mh:]
        keep[:, at] = jnp.where(r == 0, low, high)
        give[:, at] = jnp.where(r == 0, high, low).astype(jnp.bfloat16)
        swap(n).start()

    for n in range(nchunks):
        swap(n).wait_recv()
        at = slice(n * nc, (n + 1) * nc)
        total = (keep[:, at] + got[:, at].astype(jnp.float32)).astype(jnp.bfloat16)
        back[:, :, at] = total.reshape(blks, CAP, nc)
        keep_back(n).start()

        @pl.loop(1, blks)
        def _(i):
            send_back(n, lax.rem(b + i, blks)).start()

    weights = weight_buf[...]
    for n in range(nchunks):
        at = slice(n * nc, (n + 1) * nc)

        @pl.loop(0, blks)
        def _(bb):
            ref = returned.at[bb, :, pl.ds(n * nc, nc)]
            pltpu.make_async_copy(ref, ref, brecv.at[n, bb]).wait()

        acc = jnp.zeros((t_count, nc), jnp.float32)
        for e in range(experts):
            value = returned[e * group, :, at].astype(jnp.float32)
            for i in range(1, group):
                value = value + returned[e * group + i, :, at].astype(jnp.float32)
            for c in range(CAP):
                j = e * CAP + c
                acc = acc + weights[:, j : j + 1] * value[c : c + 1, :]
        out_ref[:, at] = acc.astype(jnp.bfloat16)

    @pl.loop(0, experts)
    def _(e):
        @pl.loop(0, half)
        def _(h):
            dst, copy = first(e, h)

            @pl.when(dst != b)
            def _():
                copy.wait_send()

    @pl.loop(0, quads)
    def _(i):
        forward(2 * i + parity, ysend, other, r).wait_send()

    @pl.loop(0, blks)
    def _(bb):
        forward(bb, fsend, b, sib).wait_send()

    for n in range(nchunks):
        swap(n).wait_send()

        @pl.loop(1, blks)
        def _(i):
            send_back(n, lax.rem(b + i, blks)).wait_send()


def shards(tokens, router_scores, expert_ids, gate_weight, up_weight, down_weight):
    blks = lax.axis_size("blk")
    reps = lax.axis_size("rep")
    t_count, width = tokens.shape
    units = gate_weight.shape[1]
    experts = blks * reps * units // FF
    kchunks, nchunks = 4, 4
    bf16, f32 = jnp.bfloat16, jnp.float32
    dma = pltpu.SemaphoreType.DMA
    vmem = pl.BlockSpec(memory_space=pltpu.VMEM)
    hbm = pl.BlockSpec(memory_space=pl.ANY)
    in_hbm = lambda array: pltpu.with_memory_space_constraint(array, pltpu.HBM)
    row_bytes = 2 * width
    limit = (
        3 * units * row_bytes
        + (2 * t_count + 12 * blks * CAP + experts * CAP) * row_bytes
        + (8 << 20)
    )
    return pl.pallas_call(
        functools.partial(kernel, blks, reps, experts, kchunks, nchunks),
        out_shape=jax.ShapeDtypeStruct((t_count, width), bf16),
        in_specs=[hbm] * 6,
        out_specs=vmem,
        scratch_shapes=[
            pltpu.VMEM(router_scores.shape[::-1], f32),
            pltpu.VMEM(expert_ids.shape[::-1], jnp.int32),
            pltpu.VMEM((t_count, width), bf16),
            pltpu.VMEM((width, units), bf16),
            pltpu.VMEM((width, units), bf16),
            pltpu.VMEM((units, width), bf16),
            pltpu.VMEM((experts, CAP, width), bf16),
            pltpu.VMEM((reps, blks, CAP, width), bf16),
            pltpu.VMEM((blks * CAP, width), f32),
            pltpu.VMEM((blks * CAP, width), bf16),
            pltpu.VMEM((blks * CAP, width), bf16),
            pltpu.VMEM((blks, CAP, width), bf16),
            pltpu.VMEM((blks, CAP, width), bf16),
            pltpu.VMEM((t_count, experts * CAP), f32),
            dma((2,)),
            dma(()),
            dma((2, kchunks)),
            dma((nchunks,)),
            dma((blks // 2,)),
            dma((reps, blks)),
            dma((blks,)),
            dma((blks,)),
            dma((nchunks,)),
            dma((nchunks,)),
            dma((nchunks, blks)),
            dma((nchunks, blks)),
        ],
        compiler_params=pltpu.CompilerParams(
            collective_id=0, has_side_effects=True, vmem_limit_bytes=limit
        ),
    )(
        *map(
            in_hbm,
            (router_scores.T, expert_ids.T, tokens, gate_weight, up_weight, down_weight),
        )
    )


def solution(mesh):
    placed = (
        P(("groups", "blk", "rep"), None),
        P(("groups", "blk", "rep"), None),
        P(("groups", "blk", "rep"), None),
        P(None, ("blk", "rep")),
        P(None, ("blk", "rep")),
        P(("blk", "rep"), None),
    )
    return jax.shard_map(
        shards,
        mesh=mesh,
        in_specs=placed,
        out_specs=P(("groups", "blk", "rep"), None),
        check_vma=False,
    )
```

profile of v0, /device:TPU:0, one launch (start us, length us, event | category | flops | bytes accessed | tf_op | source)
XLA Modules:
  0.0 28.4 jit_solution(14295834178237000763)
XLA Ops:
  0.0 27.4 %shard_map.64 = bf16[64,7168]{1,0:T(8,128)(2,1)S(1)} custom-call(f32[8,64]{1,0:T(8,128)} %bitcast.2, s32[8,64]{1,0:T(8,128)} %bitcast.3, bf16[64,7168]{1,0:T(8,128)(2,1)} %tok_hbm.1, bf16[7168,256]{1,0:T(8,128)(2,1)} %gate_hbm.1, bf16[7168,256]{1,0:T(8,128)(2,1)} %up_hbm.1, bf16[256,7168]{1,0:T(8,128)(2,1)} %down_hbm.1), custom_call_target="tpu_custom_call" | custom-call | tf_op jit(solution)/shard_map/pallas_call | solution.py:280
  27.5 0.9 %copy.8 = bf16[64,7168]{1,0:T(8,128)(2,1)} copy(bf16[64,7168]{1,0:T(8,128)(2,1)S(1)} %shard_map.64) | data formatting | bytes 1835008
where the time goes:
time: 28.5 us; the launch traced here: 28.4 us
  Pallas kernels  27.4 us (96%)
  local copies, waits for them, and re-layouts  0.93 us (3%)
    pallas_call x1, Pallas kernels, shards(): pl.pallas_call(functools.partial(kernel, blks, reps, experts, kchunks, nc...  27.4 us
    unnamed x1, local copies, waits for them, and re-layouts  0.93 us

commit v1 on v0

--- a/solution.py
+++ b/solution.py
@@ -69,11 +69,6 @@
         at = pl.ds(n * nc, nc)
         return pltpu.make_async_copy(down_hbm.at[:, at], wd.at[:, at], d_sem.at[n])
 
-    for k in range(kchunks):
-        for copy in k_copies(k):
-            copy.start()
-    for n in range(nchunks):
-        d_copy(n).start()
 
     for copy in route_copies:
         copy.wait()
@@ -126,6 +121,11 @@
             def _():
                 copy.start()
 
+    for k in range(kchunks):
+        for copy in k_copies(k):
+            copy.start()
+    for n in range(nchunks):
+        d_copy(n).start()
     slot_weight = placed * weight
     for j in range(slots):
         spread = jnp.where(row_i == col_i, slot_weight[j : j + 1, :], 0.0)
@@ -265,7 +265,7 @@
     t_count, width = tokens.shape
     units = gate_weight.shape[1]
     experts = blks * reps * units // FF
-    kchunks, nchunks = 4, 4
+    kchunks, nchunks = 4, 2
     bf16, f32 = jnp.bfloat16, jnp.float32
     dma = pltpu.SemaphoreType.DMA
     vmem = pl.BlockSpec(memory_space=pltpu.VMEM)

time: 28.5 us -> 25.2 us (0.88)
  Pallas kernels: 27.4 us -> 24.1 us
    pallas_call x1, Pallas kernels: 27.4 us -> 24.1 us  [shards(): pl.pallas_call(functools.partial(kernel, blks, reps, experts, kchunks, nc...]
where the time goes in v1:
time: 25.2 us; the launch traced here: 25 us
  Pallas kernels  24.1 us (96%)
  local copies, waits for them, and re-layouts  0.93 us (4%)
    pallas_call x1, Pallas kernels, shards(): pl.pallas_call(functools.partial(kernel, blks, reps, experts, kchunks, nc...  24.1 us
    unnamed x1, local copies, waits for them, and re-layouts  0.93 us

profile of v1, /device:TPU:0, one launch (start us, length us, event | category | flops | bytes accessed | tf_op | source)
XLA Modules:
  0.0 25.0 jit_solution(3708023831343781906)
XLA Ops:
  0.0 24.1 %shard_map.64 = bf16[64,7168]{1,0:T(8,128)(2,1)S(1)} custom-call(f32[8,64]{1,0:T(8,128)} %bitcast.2, s32[8,64]{1,0:T(8,128)} %bitcast.3, bf16[64,7168]{1,0:T(8,128)(2,1)} %tok_hbm.1, bf16[7168,256]{1,0:T(8,128)(2,1)} %gate_hbm.1, bf16[7168,256]{1,0:T(8,128)(2,1)} %up_hbm.1, bf16[256,7168]{1,0:T(8,128)(2,1)} %down_hbm.1), custom_call_target="tpu_custom_call" | custom-call | tf_op jit(solution)/shard_map/pallas_call | solution.py:280
  24.1 0.9 %copy.8 = bf16[64,7168]{1,0:T(8,128)(2,1)} copy(bf16[64,7168]{1,0:T(8,128)(2,1)S(1)} %shard_map.64) | data formatting | bytes 1835008
